TPU v7x, 256 devices: a whole 4x4x8 slice. The times are simulated.
256 devices in a mesh: seq: 16 (over y_hi, z), head: 16 (over y_lo, x, core).
Axes of the slice: x: 4, y: 4 (y_hi: 2, y_lo: 2; y = y_hi * 2 + y_lo), z: 8, core: 2. Of those that a mesh axis runs over, the one named last changes fastest.
Arguments:
- queries: bfloat16 [16384, 4096], P(('seq', 'head')), may hold values from -9 to 9, as said below
- keys: bfloat16 [16384, 512], P(('seq', 'head')), may hold values from -9 to 9, as said below
- values: bfloat16 [16384, 512], P(('seq', 'head')), may hold values from -6 to 6
Outputs:
- attended: bfloat16 [16384, 4096], P(('seq', 'head'))
Inputs may be any that keep to these rules, and one draw needn't show every extreme that they name: `queries`: query entries are of order one except on a few rows. `keys`: key entries are of order one except on a few rows.
All inputs are finite; a program needn't handle non-finite values.
Results may differ from a plain program's by a relative error of at most 0.005.
Values may be sent and summed in bfloat16 or wider, within the bound.
A program may use at most 64 MiB of HBM per device.

v0:
```python
import functools
import math

import jax
import jax.numpy as jnp
from jax import lax
from jax.experimental import pallas as pl
from jax.experimental.pallas import tpu as pltpu
from jax.sharding import PartitionSpec as P

H = 32
KV = 4
DH = 128
GROUP = H // KV
PLANE = 8
Z, X, Y, DK, DV, C0 = 0, 2, 4, 6, 7, 8
KINDS = C0 + 4


def kernel(n_head, planes, q_hbm, k_hbm, v_hbm, o_ref, kv, q, mx, tot, acc, lsem, send, recv):
    tok = k_hbm.shape[0]
    me = lax.axis_index("seq") * n_head + lax.axis_index("head")
    core = lax.rem(me, 2)
    x = lax.rem(lax.div(me, 2), 2)
    y = lax.rem(lax.div(me, 4), 2)
    z = lax.div(me, PLANE)

    def dev(linear):
        return (lax.div(linear, n_head), lax.rem(linear, n_head))

    to_x = dev(me + 2 - 4 * x)
    to_y = dev(me + 4 - 8 * y)
    to_core = dev(me + 1 - 2 * core)
    up = dev(lax.min(me + PLANE, planes * PLANE - 1))
    down = dev(lax.max(me - PLANE, 0))

    own_k = pltpu.make_async_copy(k_hbm, kv.at[me, 0], lsem.at[0])
    own_v = pltpu.make_async_copy(v_hbm, kv.at[me, 1], lsem.at[1])
    own_q = pltpu.make_async_copy(q_hbm, q, lsem.at[2])
    own_k.start()
    own_v.start()
    own_q.start()

    barrier = pltpu.get_barrier_semaphore()

    def greet(where):
        pl.semaphore_signal(barrier, inc=1, device_id=where, device_id_type=pl.DeviceIdType.MESH)

    greet(to_x)
    greet(to_y)
    greet(to_core)

    @pl.when(z < planes - 1)
    def _():
        greet(up)

    @pl.when(z > 0)
    def _():
        greet(down)

    pl.semaphore_wait(barrier, 3 + lax.min(z, 1) + lax.min(planes - 1 - z, 1))

    own_k.wait()
    own_v.wait()

    def slot(k, yy, xx, cc):
        return (z - k) * PLANE + yy * 4 + xx * 2 + cc

    def copy(kind, k, where, block, half=None, later=0):
        ref = kv.at[block] if half is None else kv.at[block, half]
        return pltpu.make_async_remote_copy(
            src_ref=ref,
            dst_ref=ref,
            send_sem=send.at[kind, k],
            recv_sem=recv.at[kind, k + later],
            device_id=where,
            device_id_type=pl.DeviceIdType.MESH,
        )

    def out_z(k, half):
        return copy(Z + half, k, up, slot(k, y, x, core), half, later=1)

    def outs(k):
        mine, xs, ys, diag = (
            slot(k, y, x, core),
            slot(k, y, 1 - x, core),
            slot(k, 1 - y, x, core),
            slot(k, 1 - y, 1 - x, core),
        )
        return dict(
            xk=lambda: copy(X, k, to_x, mine, 0),
            xv=lambda: copy(X + 1, k, to_x, mine, 1),
            yk=lambda: copy(Y, k, to_y, mine, 0),
            yv=lambda: copy(Y + 1, k, to_y, mine, 1),
            dk=lambda: copy(DK, k, to_y, xs, 0),
            dv=lambda: copy(DV, k, to_x, ys, 1),
            c0=lambda: copy(C0, k, to_core, mine),
            c1=lambda: copy(C0 + 1, k, to_core, xs),
            c2=lambda: copy(C0 + 2, k, to_core, ys),
            c3=lambda: copy(C0 + 3, k, to_core, diag),
        )

    def landed(kind, k, block, half=None):
        copy(kind, k, to_x, block, half).wait_recv()

    def send_up(k, half):
        @pl.when(z < planes - 1)
        def _():
            out_z(k, half).start()

    scale = math.log2(math.e) / math.sqrt(DH)
    rows = GROUP * tok

    def chunk(k, first, heads=range(KV), side=None):
        blocks = PLANE if side is None else PLANE // 2
        base = (z - k) * PLANE + (0 if side is None else side * blocks)
        width = blocks * tok
        for g in heads:
            cols = slice(g * DH, (g + 1) * DH)
            kk = kv[pl.ds(base, blocks), 0, :, cols].reshape(width, DH)
            vv = kv[pl.ds(base, blocks), 1, :, cols].reshape(width, DH)
            qq = jnp.concatenate(
                [q[:, (g * GROUP + h) * DH : (g * GROUP + h + 1) * DH] for h in range(GROUP)], axis=0
            )
            s = lax.dot_general(
                kk, qq, (((1,), (1,)), ((), ())), preferred_element_type=jnp.float32
            )
            if first:
                key = lax.broadcasted_iota(jnp.int32, (width, rows), 0)
                row = lax.rem(lax.broadcasted_iota(jnp.int32, (width, rows), 1), tok)
                s = jnp.where(key <= row + lax.rem(me, PLANE) * tok, s, -jnp.inf)
            top = jnp.max(s, axis=0, keepdims=True)
            if not first:
                old = mx[g]
                top = jnp.maximum(old, top)
            p = jnp.exp2((s - top) * scale)
            total = jnp.sum(p, axis=0, keepdims=True)
            pv = lax.dot_general(
                vv,
                p.astype(jnp.bfloat16),
                (((0,), (0,)), ((), ())),
                preferred_element_type=jnp.float32,
            )
            if not first:
                factor = jnp.exp2((old - top) * scale)
                total += tot[g] * factor
                pv += acc[g] * factor
            acc[g] = pv
            tot[g] = total
            mx[g] = top

    def relay_first(k):
        o = outs(k)

        @pl.when(k < z)
        def _():
            landed(Z, k + 1, slot(k + 1, y, x, core), 0)
            send_up(k + 1, 0)
            outs(k + 1)["xk"]().start()

        landed(X, k, slot(k, y, 1 - x, core), 0)
        o["dk"]().start()
        landed(Y + 1, k, slot(k, 1 - y, x, core), 1)
        o["dv"]().start()

    def relay_mid(k):
        o = outs(k)

        @pl.when(k < z)
        def _():
            landed(Z + 1, k + 1, slot(k + 1, y, x, core), 1)
            send_up(k + 1, 1)
            later = outs(k + 1)
            later["yv"]().start()
            later["xv"]().start()
            later["yk"]().start()
            later["c0"]().start()

        landed(X + 1, k, slot(k, y, 1 - x, core), 1)
        o["c1"]().start()
        landed(Y, k, slot(k, 1 - y, x, core), 0)
        o["c2"]().start()

    def relay_second(k):
        diag = slot(k, 1 - y, 1 - x, core)
        landed(DK, k, diag, 0)
        landed(DV, k, diag, 1)
        outs(k)["c3"]().start()

    def relay_near(k):
        landed(C0, k, slot(k, y, x, 1 - core))
        landed(C0 + 1, k, slot(k, y, 1 - x, 1 - core))

    def relay_far(k):
        landed(C0 + 2, k, slot(k, 1 - y, x, 1 - core))
        landed(C0 + 3, k, slot(k, 1 - y, 1 - x, 1 - core))

    o = outs(0)
    for half in (0, 1):
        send_up(0, half)
    for name in ("xk", "yv", "xv", "yk", "c0"):
        o[name]().start()
    own_q.wait()
    relay_first(0)
    relay_mid(0)
    relay_second(0)
    relay_near(0)
    relay_far(0)

    @pl.when(z > 0)
    def _():
        relay_first(1)
        chunk(0, True, (0, 1))
        relay_mid(1)
        chunk(0, True, (2, 3))
        relay_second(1)

    @pl.when(z == 0)
    def _():
        chunk(0, True)

    def body(k, carry):
        relay_near(k - 1)
        relay_far(k - 1)
        relay_first(k)
        chunk(k - 1, False, (0, 1))
        relay_mid(k)
        chunk(k - 1, False, (2, 3))
        relay_second(k)
        return carry

    lax.fori_loop(2, z + 1, body, 0)

    @pl.when(z > 0)
    def _():
        relay_near(z)
        chunk(z, False, side=y)
        relay_far(z)
        chunk(z, False, side=1 - y)

    for g in range(KV):
        out = (acc[g] / tot[g]).T.astype(o_ref.dtype)
        for h in range(GROUP):
            o_ref[:, (g * GROUP + h) * DH : (g * GROUP + h + 1) * DH] = out[h * tok : (h + 1) * tok]

    def drain(k, carry):
        @pl.when(z < planes - 1)
        def _():
            for half in (0, 1):
                out_z(k, half).wait_send()

        for c in outs(k).values():
            c().wait_send()
        return carry

    lax.fori_loop(0, z + 1, drain, 0)


def per_device(queries, keys, values):
    n_head = lax.axis_size("head")
    devices = n_head * lax.axis_size("seq")
    planes = devices // PLANE
    tok = queries.shape[0]
    rows = GROUP * tok
    hbm = pl.BlockSpec(memory_space=pl.ANY)
    return pl.pallas_call(
        functools.partial(kernel, n_head, planes),
        out_shape=pltpu.VMEM(queries.shape, queries.dtype),
        in_specs=[hbm] * 3,
        out_specs=pl.BlockSpec(memory_space=pltpu.VMEM),
        scratch_shapes=[
            pltpu.VMEM((devices, 2, tok, KV * DH), jnp.bfloat16),
            pltpu.VMEM(queries.shape, jnp.bfloat16),
            pltpu.VMEM((KV, 1, rows), jnp.float32),
            pltpu.VMEM((KV, 1, rows), jnp.float32),
            pltpu.VMEM((KV, DH, rows), jnp.float32),
            pltpu.SemaphoreType.DMA((3,)),
            pltpu.SemaphoreType.DMA((KINDS, planes)),
            pltpu.SemaphoreType.DMA((KINDS, planes)),
        ],
        compiler_params=pltpu.CompilerParams(
            collective_id=0, has_side_effects=True, vmem_limit_bytes=60 * 1024 * 1024
        ),
        name="relay_attention",
    )(queries, keys, values)


def solution(mesh):
    spec = P(("seq", "head"), None)
    return jax.shard_map(
        per_device, mesh=mesh, in_specs=(spec, spec, spec), out_specs=spec, check_vma=False
    )
```

profile of v0, /device:TPU:249, one launch (start us, length us, event | category | flops | bytes accessed | tf_op | source)
XLA Modules:
  0.0 285.2 jit_solution(12656627119769398054)
XLA Ops:
  0.0 284.4 %relay_attention.1 = bf16[64,4096]{1,0:T(8,128)(2,1)S(1)} custom-call(bf16[64,4096]{1,0:T(8,128)(2,1)} %q_hbm.1, bf16[64,512]{1,0:T(8,128)(2,1)} %k_hbm.1, bf16[64,512]{1,0:T(8,128)(2,1)} %v_hbm.1), custom_call_target="tpu_custom_call" | custom-call | tf_op jit(solution)/shard_map/relay_attention/pallas_call | solution.py:266
  284.4 0.8 copy.5
where the time goes:
time: 285 us
  Pallas kernels  284 us (100%)
    pallas_call x1, Pallas kernels, per_device(): pl.pallas_call(functools.partial(kernel, n_head, planes), out_shape=pltpu...  284 us

commit v1 on v0

v1 whole, which is shorter than its diff:
```python
import functools
import math

import jax
import jax.numpy as jnp
from jax import lax
from jax.experimental import pallas as pl
from jax.experimental.pallas import tpu as pltpu
from jax.sharding import PartitionSpec as P

H = 32
KV = 4
DH = 128
GROUP = H // KV
NX, NY, NZ = 4, 4, 8
TILES = 8
SLAB = 1024
CHUNK = 256
SCALE = math.log2(math.e) / math.sqrt(DH)
ZI_OF = (0, 2, 1, 3)
f32 = jnp.float32
bf16 = jnp.bfloat16


def rem(a, b):
    return lax.rem(a, jnp.int32(b))


def div(a, b):
    return lax.div(a, jnp.int32(b))


def tie(z):
    return rem(z + 6 + 4 * rem(div(z, 2), 2), NZ)


def zsrc(z, zi):
    far = rem(z + 6 + 4 * rem(div(z, 2), 2), NZ)
    near = jnp.where(zi == 0, z, jnp.where(zi == 1, rem(z + 1, NZ), rem(z + 7, NZ)))
    return jnp.where(zi == 3, far, near)


def device(x, y, z, c):
    return (div(y, 2) * NZ + z, rem(y, 2) * 8 + x * 2 + c)


def kernel(
    q_hbm, k_hbm, v_hbm, o_ref, kv, q_own, k_own, v_own, q_in, qt, o_stage, mx, tot, acc, s_buf,
    lsem, zsend, zrecv, qsend, qrecv, gsend, grecv, csend, crecv, osend, orecv,
):
    seq = lax.axis_index("seq")
    head = lax.axis_index("head")
    yhi = div(seq, NZ)
    z = rem(seq, NZ)
    ylo = div(head, 8)
    x = rem(div(head, 2), 4)
    c = rem(head, 2)
    y = yhi * 2 + ylo
    oc = 1 - c
    oy = 3 - y
    blk = ylo * 4 + x
    kind = rem(z, KV)

    def remote(src, dst, ssem, rsem, where):
        return pltpu.make_async_remote_copy(
            src_ref=src, dst_ref=dst, send_sem=ssem, recv_sem=rsem,
            device_id=where, device_id_type=pl.DeviceIdType.MESH,
        )

    def local(src, dst, sem):
        return pltpu.make_async_copy(src, dst, sem)

    loads = [
        local(k_hbm, k_own, lsem.at[0]), local(v_hbm, v_own, lsem.at[1]), local(q_hbm, q_own, lsem.at[2]),
    ]
    for load in loads:
        load.start()

    def kv_cols(zz):
        return pl.ds(pl.multiple_of(rem(zz, KV) * DH, DH), DH)

    kept = [
        local(k_hbm.at[:, kv_cols(z)], kv.at[0, yhi, z, blk, c], lsem.at[3]),
        local(v_hbm.at[:, kv_cols(z)], kv.at[1, yhi, z, blk, c], lsem.at[4]),
    ]
    for load in kept:
        load.start()

    tz = [z, rem(z + 1, NZ), rem(z + 7, NZ), tie(z)]
    cs = (c, oc)
    ys = (y, oy)

    barrier = pltpu.get_barrier_semaphore()

    def greet(where):
        pl.semaphore_signal(barrier, inc=1, device_id=where, device_id_type=pl.DeviceIdType.MESH)

    greeted = 0
    for j in range(4):
        for yy in range(2):
            for k in range(2):
                if j or yy or k:
                    greet(device(x, ys[yy], tz[j], cs[k]))
                    greeted += 1
    for zz in (rem(z + 3, NZ), rem(z + 4, NZ), rem(z + 5, NZ), rem(2 * z + NZ - tz[3], NZ)):
        greet(device(x, y, zz, c))
        greeted += 1
    for where in (
        device(rem(x + 1, NX), y, z, c), device(rem(x + 3, NX), y, z, c), device(x, yhi * 2 + 1 - ylo, z, c),
    ):
        greet(where)
        greeted += 1

    for load in loads:
        load.wait()
    pl.semaphore_wait(barrier, greeted)

    own = (k_own, v_own)

    def z_copy(dz, n):
        zz = rem(z + dz, NZ)
        return remote(
            own[n].at[:, kv_cols(zz)], kv.at[n, yhi, z, blk, c], zsend.at[n, dz], zrecv.at[n, dz], device(x, y, zz, c)
        )

    def z_landed(dz, n):
        zz = rem(z + NZ - dz, NZ)
        remote(
            own[n].at[:, kv_cols(z)], kv.at[n, yhi, zz, blk, c], zsend.at[n, dz], zrecv.at[n, dz], device(x, y, zz, c)
        ).wait_recv()

    z_order = (4, 3, 5, 2, 6, 1, 7)
    for dz in z_order:
        for n in range(2):
            z_copy(dz, n).start()
    for load in kept:
        load.wait()

    def q_cols(j, yy, k):
        yh = div(ys[yy], 2)
        first = rem(tz[j], KV) * GROUP + 4 * yh + 2 * cs[k]
        return pl.ds(pl.multiple_of(first * DH, 2 * DH), 2 * DH)

    def q_copy(j, yy, k):
        tile = yy * 4 + ZI_OF[j]
        return remote(
            q_own.at[:, q_cols(j, yy, k)], q_in.at[tile, c], qsend.at[(j * 2 + yy) * 2 + k], qrecv.at[tile, c],
            device(x, ys[yy], tz[j], cs[k]),
        )

    def q_landed(tile, k):
        yy, zi = divmod(tile, 4)
        zz = (z, tz[1], tz[2], tz[3])[zi]
        remote(
            q_own.at[:, pl.ds(0, 2 * DH)], q_in.at[tile, cs[k]], qsend.at[0], qrecv.at[tile, cs[k]],
            device(x, ys[yy], zz, cs[k]),
        ).wait_recv()

    for yy in (1, 0):
        for j in (3, 1, 2, 0):
            for k in range(2):
                if j or yy or k:
                    q_copy(j, yy, k).start()
    q_in[0, c] = q_own[:, q_cols(0, 0, 0)]

    for dz in z_order:
        for n in range(2):
            z_landed(dz, n)

    def a_dev(d):
        return device(rem(x + d * (1 - c), NX), rem(y + d * c, NY), z, c)

    def b_dev(d):
        return device(rem(x + d * c, NX), rem(y + d * (1 - c), NY), z, c)

    def block(ra, rb):
        xk = rem(x + ra * (1 - c) + rb * c, NX)
        yk = rem(y + ra * c + rb * (1 - c), NY)
        return div(yk, 2), rem(yk, 2) * 4 + xk

    def piece(ra, rb, n, core):
        yh, q = block(ra, rb)
        if n is None:
            return kv.at[:, yh, :, q, core]
        return kv.at[n, yh, :, q, core]

    def g_copy(index, ra, rb, n, axis, d):
        ref = piece(ra, rb, n, c)
        to = a_dev(d % 4) if axis == 0 else b_dev(d % 4)
        if axis == 0:
            there = ((ra - d) % 4, rb)
        else:
            there = (ra, (rb - d) % 4)
        return remote(ref, ref, gsend.at[index], grecv.at[there[0], there[1], n or 0], to)

    def g_landed(ra, rb, n):
        ref = piece(ra, rb, n, c)
        remote(ref, ref, gsend.at[0], grecv.at[ra, rb, n or 0], a_dev(1)).wait_recv()

    def c_copy(ra, rb):
        yh, q = block(ra, rb)
        ref = piece(ra, rb, None, c)
        return remote(ref, ref, csend.at[yh, q], crecv.at[yh, q], device(x, y, z, oc))

    sends = []

    def send(copy):
        copy.start()
        sends.append(copy)

    def g_send(*what):
        send(g_copy(len(g_list), *what))
        g_list.append(what)

    g_list = []

    def spread(ra, rb, axis):
        for d in (1, -1):
            g_send(ra, rb, None, axis, d)

    spread(0, 0, 0)
    spread(0, 0, 1)
    send(c_copy(0, 0))

    def line(ra, rb, axis, then):
        for d, n in ((1, 0), (-1, 1)):
            here = ((ra - d) % 4, rb) if axis == 0 else (ra, (rb - d) % 4)
            g_landed(*here, None)
            g_send(*here, n, axis, d)
            if then:
                spread(*here, 1)
            send(c_copy(*here))
        far = ((ra + 2) % 4, rb) if axis == 0 else (ra, (rb + 2) % 4)
        return far

    def far_landed(far, then):
        g_landed(*far, 0)
        g_landed(*far, 1)
        if then:
            spread(*far, 1)
        send(c_copy(*far))

    far_a = line(0, 0, 0, True)
    far_b = line(0, 0, 1, False)
    far_landed(far_a, True)
    far_landed(far_b, False)
    for ra in (3, 1, 2):
        far_landed(line(ra, 0, 1, False), False)

    for yh in range(2):
        for q in range(8):
            ref = kv.at[:, yh, :, q, oc]
            remote(ref, ref, csend.at[yh, q], crecv.at[yh, q], device(x, y, z, oc)).wait_recv()

    for tile in range(TILES):
        for k in range(2):
            if tile or k:
                q_landed(tile, k)
        for h in range(2):
            part = q_in[tile, :, :, h * DH : (h + 1) * DH].reshape(2 * 64, DH)
            qt[tile, :, h * DH : (h + 1) * DH] = part.T
    mx[...] = jnp.full(mx.shape, -jnp.inf, f32)
    tot[...] = jnp.zeros(tot.shape, f32)
    acc[...] = jnp.zeros(acc.shape, f32)

    def last_slab(t):
        side = jnp.where(t < 4, yhi, 1 - yhi)
        return side * NZ + zsrc(z, rem(t, 4))

    def segment(n, s, g):
        yh = div(s, NZ)
        zz = rem(s, NZ)
        return jnp.concatenate([kv[n, yh, zz, 2 * g + i].reshape(2 * 64, DH) for i in range(2)], axis=0)

    def fold(v, op):
        return op(v.reshape(v.shape[0] // 8, 8, v.shape[1]), axis=0)

    def score(t, s, g, slot, masked):
        sc = lax.dot_general(
            segment(0, s, g), qt[t], (((1,), (0,)), ((), ())), preferred_element_type=f32
        )
        if masked:
            yl = jnp.where(t < 4, ylo, 1 - ylo)
            row = rem(lax.broadcasted_iota(jnp.int32, sc.shape, 1), 128) + (yl * 4 + x) * 128
            key = lax.broadcasted_iota(jnp.int32, sc.shape, 0) + g * CHUNK
            sc = jnp.where(key <= row, sc, -jnp.inf)
        s_buf[slot, g * CHUNK : (g + 1) * CHUNK] = sc
        return fold(sc, jnp.max)

    def apply(s, g, slot, top8, l8, pv):
        sc = s_buf[slot, g * CHUNK : (g + 1) * CHUNK].reshape(CHUNK // 8, 8, 2 * DH)
        p = jnp.exp2((sc - top8[None]) * SCALE)
        l8 = l8 + jnp.sum(p, axis=0)
        d = lax.dot_general(
            segment(1, s, g), p.reshape(CHUNK, 2 * DH).astype(bf16), (((0,), (0,)), ((), ())),
            preferred_element_type=f32,
        )
        return l8, (d if pv is None else pv + d)

    parts = SLAB // CHUNK

    def o_cols(t):
        return pl.ds(pl.multiple_of((kind * GROUP + 4 * yhi + 2 * c) * DH, 2 * DH), 2 * DH)

    def o_copy(t, k):
        cc = k
        yy = jnp.where(t < 4, y, oy)
        zz = zsrc(z, rem(t, 4))
        return remote(
            o_stage.at[t, cc], o_ref.at[:, o_cols(t)], osend.at[t, cc],
            orecv.at[t, c], device(x, yy, zz, cc),
        )

    def finish(t):
        for h in range(2):
            cols = slice(h * DH, (h + 1) * DH)
            whole = jnp.sum(tot[t, :, cols], axis=0, keepdims=True)
            rows = (acc[t, :, cols] / whole).T.astype(bf16)
            o_stage[t, :, :, cols] = rows.reshape(2, 64, DH)

        for k in range(2):
            @pl.when((t != 0) | (c != k))
            def _():
                o_copy(t, k).start()

    def prep(t, m8):
        old = mx[t]
        top = jnp.maximum(old, jnp.max(m8, axis=0, keepdims=True))
        factor = jnp.exp2((old - top) * SCALE)
        mx[t] = top
        return jnp.broadcast_to(top, (8, 2 * DH)), factor

    def item(t, s, tn, sn, m8, u, masked):
        top8, factor = prep(t, m8)
        l8, pv, nm = tot[t] * factor, None, None
        for g in range(parts):
            r = score(tn, sn, g, 1 - u, masked)
            nm = r if nm is None else jnp.maximum(nm, r)
            l8, pv = apply(s, g, u, top8, l8, pv)
        acc[t] = acc[t] * factor + pv
        tot[t] = l8
        return nm

    count = 0
    for t in range(TILES):
        count = count + last_slab(jnp.int32(t)) + 1

    def first(t, s, masked):
        m8 = None
        for g in range(parts):
            r = score(t, s, g, 0, masked)
            m8 = r if m8 is None else jnp.maximum(m8, r)
        return m8

    zero = jnp.int32(0)
    m8 = lax.cond(last_slab(zero) == 0, lambda: first(zero, zero, True), lambda: first(zero, zero, False))

    def pair(i, carry):
        t, s, m8 = carry
        for u in range(2):
            done = s == last_slab(t)
            tn = jnp.where(done, lax.min(t + 1, TILES - 1), t)
            sn = jnp.where(done, 0, s + 1)
            m8 = lax.cond(
                sn == last_slab(tn),
                lambda m8=m8, u=u, t=t, s=s, tn=tn, sn=sn: item(t, s, tn, sn, m8, u, True),
                lambda m8=m8, u=u, t=t, s=s, tn=tn, sn=sn: item(t, s, tn, sn, m8, u, False),
            )

            @pl.when(done)
            def _(t=t):
                finish(t)

            t, s = tn, sn
        return t, s, m8

    lax.fori_loop(0, div(count, 2), pair, (zero, zero, m8))
    o_ref[:, o_cols(0)] = o_stage[0, c]

    for tile in range(TILES):
        for k in range(2):
            @pl.when((tile != 0) | (c != k))
            def _(tile=tile, k=k):
                o_copy(jnp.int32(tile), k).wait_send()

    for j in range(4):
        for yy in range(2):
            for k in range(2):
                if j or yy or k:
                    tile = yy * 4 + ZI_OF[j]
                    first_head = rem(tz[j], KV) * GROUP + 4 * div(ys[yy], 2) + 2 * cs[k]
                    cols = pl.ds(pl.multiple_of(first_head * DH, 2 * DH), 2 * DH)
                    remote(
                        o_stage.at[tile, c], o_ref.at[:, cols], osend.at[tile, c], orecv.at[tile, cs[k]],
                        device(x, ys[yy], tz[j], cs[k]),
                    ).wait_recv()
    for copy in sends:
        copy.wait_send()
    for dz in z_order:
        for n in range(2):
            z_copy(dz, n).wait_send()
    for yy in (1, 0):
        for j in range(4):
            for k in range(2):
                if j or yy or k:
                    q_copy(j, yy, k).wait_send()


def per_device(queries, keys, values):
    hbm = pl.BlockSpec(memory_space=pl.ANY)
    dma = pltpu.SemaphoreType.DMA
    return pl.pallas_call(
        kernel,
        out_shape=pltpu.VMEM(queries.shape, queries.dtype),
        in_specs=[hbm] * 3,
        out_specs=pl.BlockSpec(memory_space=pltpu.VMEM),
        scratch_shapes=[
            pltpu.VMEM((2, 2, NZ, 8, 2, 64, DH), bf16),
            pltpu.VMEM(queries.shape, bf16),
            pltpu.VMEM(keys.shape, bf16),
            pltpu.VMEM(values.shape, bf16),
            pltpu.VMEM((TILES, 2, 64, 2 * DH), bf16),
            pltpu.VMEM((TILES, DH, 2 * DH), bf16),
            pltpu.VMEM((TILES, 2, 64, 2 * DH), bf16),
            pltpu.VMEM((TILES, 1, 2 * DH), f32),
            pltpu.VMEM((TILES, 8, 2 * DH), f32),
            pltpu.VMEM((TILES, DH, 2 * DH), f32),
            pltpu.VMEM((2, SLAB, 2 * DH), f32),
            dma((5,)),
            dma((2, NZ)), dma((2, NZ)),
            dma((16,)), dma((TILES, 2)),
            dma((36,)), dma((4, 4, 2)),
            dma((2, 8)), dma((2, 8)),
            dma((TILES, 2)), dma((TILES, 2)),
        ],
        compiler_params=pltpu.CompilerParams(
            collective_id=0, has_side_effects=True, vmem_limit_bytes=60 * 1024 * 1024
        ),
        name="regrouped_attention",
    )(queries, keys, values)


def solution(mesh):
    spec = P(("seq", "head"), None)
    return jax.shard_map(
        per_device, mesh=mesh, in_specs=(spec, spec, spec), out_specs=spec, check_vma=False
    )
```

time: 285 us -> 91.9 us (0.32)
  the two profiles are of different devices: /device:TPU:249 before, /device:TPU:1 now
where the time goes in v1:
time: 91.9 us; the launch traced here: 91.8 us
  Pallas kernels  91 us (99%)
    pallas_call x1, Pallas kernels, per_device(): pl.pallas_call(kernel, out_shape=pltpu.VMEM(queries.shape, queries.dtype)...  91 us

profile of v1, /device:TPU:1, one launch (start us, length us, event | category | flops | bytes accessed | tf_op | source)
XLA Modules:
  0.0 91.8 jit_solution(7659521224415035942)
XLA Ops:
  0.0 91.0 %regrouped_attention.1 = bf16[64,4096]{1,0:T(8,128)(2,1)S(1)} custom-call(bf16[64,4096]{1,0:T(8,128)(2,1)} %q_hbm.1, bf16[64,512]{1,0:T(8,128)(2,1)} %k_hbm.1, bf16[64,512]{1,0:T(8,128)(2,1)} %v_hbm.1), custom_call_target="tpu_custom_call" | custom-call | tf_op jit(solution)/shard_map/regrouped_attention/pallas_call | solution.py:412
  91.0 0.8 copy.5

commit v2 on v1

--- a/solution.py
+++ b/solution.py
@@ -14,6 +14,7 @@
 GROUP = H // KV
 NX, NY, NZ = 4, 4, 8
 TILES = 8
+ROUNDS = NZ // 2
 SLAB = 1024
 CHUNK = 256
 SCALE = math.log2(math.e) / math.sqrt(DH)
@@ -120,19 +121,21 @@
     def z_copy(dz, n):
         zz = rem(z + dz, NZ)
         return remote(
-            own[n].at[:, kv_cols(zz)], kv.at[n, yhi, z, blk, c], zsend.at[n, dz], zrecv.at[n, dz], device(x, y, zz, c)
+            own[n].at[:, kv_cols(zz)], kv.at[n, yhi, z, blk, c], zsend.at[n, dz], zrecv.at[n, z], device(x, y, zz, c)
         )
 
-    def z_landed(dz, n):
-        zz = rem(z + NZ - dz, NZ)
+    def z_landed(zz, n):
         remote(
-            own[n].at[:, kv_cols(z)], kv.at[n, yhi, zz, blk, c], zsend.at[n, dz], zrecv.at[n, dz], device(x, y, zz, c)
+            own[n].at[:, kv_cols(z)], kv.at[n, yhi, zz, blk, c], zsend.at[n, 0], zrecv.at[n, zz], device(x, y, zz, c)
         ).wait_recv()
 
     z_order = (4, 3, 5, 2, 6, 1, 7)
-    for dz in z_order:
-        for n in range(2):
-            z_copy(dz, n).start()
+
+    def z_start():
+        for dz in z_order:
+            for n in range(2):
+                z_copy(dz, n).start()
+
     for load in kept:
         load.wait()
 
@@ -156,16 +159,24 @@
             device(x, ys[yy], zz, cs[k]),
         ).wait_recv()
 
-    for yy in (1, 0):
-        for j in (3, 1, 2, 0):
-            for k in range(2):
-                if j or yy or k:
-                    q_copy(j, yy, k).start()
+    def q_start():
+        for yy in (1, 0):
+            for j in (3, 1, 2, 0):
+                for k in range(2):
+                    if j or yy or k:
+                        q_copy(j, yy, k).start()
+
+    @pl.when(z < NZ // 2)
+    def _():
+        z_start()
+        q_start()
+
+    @pl.when(z >= NZ // 2)
+    def _():
+        q_start()
+        z_start()
+
     q_in[0, c] = q_own[:, q_cols(0, 0, 0)]
-
-    for dz in z_order:
-        for n in range(2):
-            z_landed(dz, n)
 
     def a_dev(d):
         return device(rem(x + d * (1 - c), NX), rem(y + d * c, NY), z, c)
@@ -178,79 +189,89 @@
         yk = rem(y + ra * c + rb * (1 - c), NY)
         return div(yk, 2), rem(yk, 2) * 4 + xk
 
-    def piece(ra, rb, n, core):
+    def piece(r, ra, rb, n, core):
         yh, q = block(ra, rb)
+        zs = pl.ds(2 * r, 2)
         if n is None:
-            return kv.at[:, yh, :, q, core]
-        return kv.at[n, yh, :, q, core]
-
-    def g_copy(index, ra, rb, n, axis, d):
-        ref = piece(ra, rb, n, c)
+            return kv.at[:, yh, zs, q, core]
+        return kv.at[n, yh, zs, q, core]
+
+    def g_copy(r, index, ra, rb, n, axis, d):
+        ref = piece(r, ra, rb, n, c)
         to = a_dev(d % 4) if axis == 0 else b_dev(d % 4)
-        if axis == 0:
-            there = ((ra - d) % 4, rb)
-        else:
-            there = (ra, (rb - d) % 4)
-        return remote(ref, ref, gsend.at[index], grecv.at[there[0], there[1], n or 0], to)
-
-    def g_landed(ra, rb, n):
-        ref = piece(ra, rb, n, c)
-        remote(ref, ref, gsend.at[0], grecv.at[ra, rb, n or 0], a_dev(1)).wait_recv()
-
-    def c_copy(ra, rb):
-        yh, q = block(ra, rb)
-        ref = piece(ra, rb, None, c)
-        return remote(ref, ref, csend.at[yh, q], crecv.at[yh, q], device(x, y, z, oc))
-
-    sends = []
-
-    def send(copy):
-        copy.start()
-        sends.append(copy)
-
-    def g_send(*what):
-        send(g_copy(len(g_list), *what))
-        g_list.append(what)
-
-    g_list = []
-
-    def spread(ra, rb, axis):
-        for d in (1, -1):
-            g_send(ra, rb, None, axis, d)
-
-    spread(0, 0, 0)
-    spread(0, 0, 1)
-    send(c_copy(0, 0))
-
-    def line(ra, rb, axis, then):
+        there = ((ra - d) % 4, rb) if axis == 0 else (ra, (rb - d) % 4)
+        return remote(ref, ref, gsend.at[r, index], grecv.at[r, there[0], there[1], n or 0], to)
+
+    def g_landed(r, ra, rb, n):
+        ref = piece(r, ra, rb, n, c)
+        remote(ref, ref, gsend.at[r, 0], grecv.at[r, ra, rb, n or 0], a_dev(1)).wait_recv()
+
+    def c_copy(r, ra, rb):
+        ref = piece(r, ra, rb, None, c)
+        return remote(ref, ref, csend.at[r, ra * 4 + rb], crecv.at[r], device(x, y, z, oc))
+
+    def both_ways(ra, rb, axis):
+        return [(ra, rb, None, axis, 1), (ra, rb, None, axis, -1)]
+
+    events = [([], both_ways(0, 0, 0) + both_ways(0, 0, 1), (0, 0))]
+    for d, n in ((1, 0), (-1, 1)):
+        ra = -d % 4
+        events.append(([(ra, 0, None)], [(ra, 0, n, 0, d)] + both_ways(ra, 0, 1), (ra, 0)))
+    for d, n in ((1, 0), (-1, 1)):
+        rb = -d % 4
+        events.append(([(0, rb, None)], [(0, rb, n, 1, d)], (0, rb)))
+    events.append(([(2, 0, 0), (2, 0, 1)], both_ways(2, 0, 1), (2, 0)))
+    events.append(([(0, 2, 0), (0, 2, 1)], [], (0, 2)))
+    for ra in (3, 1, 2):
         for d, n in ((1, 0), (-1, 1)):
-            here = ((ra - d) % 4, rb) if axis == 0 else (ra, (rb - d) % 4)
-            g_landed(*here, None)
-            g_send(*here, n, axis, d)
-            if then:
-                spread(*here, 1)
-            send(c_copy(*here))
-        far = ((ra + 2) % 4, rb) if axis == 0 else (ra, (rb + 2) % 4)
-        return far
-
-    def far_landed(far, then):
-        g_landed(*far, 0)
-        g_landed(*far, 1)
-        if then:
-            spread(*far, 1)
-        send(c_copy(*far))
-
-    far_a = line(0, 0, 0, True)
-    far_b = line(0, 0, 1, False)
-    far_landed(far_a, True)
-    far_landed(far_b, False)
-    for ra in (3, 1, 2):
-        far_landed(line(ra, 0, 1, False), False)
-
-    for yh in range(2):
-        for q in range(8):
-            ref = kv.at[:, yh, :, q, oc]
-            remote(ref, ref, csend.at[yh, q], crecv.at[yh, q], device(x, y, z, oc)).wait_recv()
+            rb = -d % 4
+            events.append(([(ra, rb, None)], [(ra, rb, n, 1, d)], (ra, rb)))
+        events.append(([(ra, 2, 0), (ra, 2, 1)], [], (ra, 2)))
+    when = (0, 7, 8, 9, 10, 17, 19, 14, 15, 22, 18, 20, 29, 27, 28, 37)
+    every = len(events)
+    span = max(when) + 1
+    numbered, total_sends = [], 0
+    for waits, outs, where in events:
+        numbered.append((waits, [(total_sends + i, o) for i, o in enumerate(outs)], where))
+        total_sends += len(outs)
+
+    def run_event(e, r):
+        waits, outs, where = numbered[e]
+        if e == 0:
+            for i in range(2):
+                zz = 2 * r + i
+
+                @pl.when(zz != z)
+                def _(zz=zz):
+                    for n in range(2):
+                        z_landed(zz, n)
+        for w in waits:
+            g_landed(r, *w)
+        for i, o in outs:
+            g_copy(r, i, *o).start()
+        c_copy(r, *where).start()
+
+    by_slot = {t % every: e for e, t in enumerate(when)}
+
+    def slot(s):
+        def case(m):
+            e = by_slot[m]
+
+            def run():
+                r = div(s - when[e], every)
+
+                @pl.when((s >= when[e]) & (r < ROUNDS))
+                def _():
+                    run_event(e, r)
+
+            return run
+
+        lax.switch(rem(s, every), [case(m) for m in range(every)])
+
+    def slots(lo, hi):
+        lax.fori_loop(lo, hi, lambda s, _: (slot(s), 0)[1], 0)
+
+    slots(0, span)
 
     for tile in range(TILES):
         for k in range(2):
@@ -341,40 +362,86 @@
         tot[t] = l8
         return nm
 
-    count = 0
-    for t in range(TILES):
-        count = count + last_slab(jnp.int32(t)) + 1
+    near = [zsrc(z, i) for i in range(4)]
+
+    def pick(i):
+        zq = near[3]
+        for k in (2, 1, 0):
+            zq = jnp.where(i == k, near[k], zq)
+        return zq
+
+    def tile_at(u):
+        return rem(u + 4 * yhi, TILES)
+
+    def steps(u, r):
+        zq = pick(rem(u, 4))
+        own_side = jnp.clip(zq - 2 * r + 1, 0, 2)
+        return own_side + jnp.where(u >= 4, 2, 0)
+
+    def following(u, r):
+        at = jnp.int32(4)
+        for k in (3, 2, 1, 0):
+            at = jnp.where((k > u) & (steps(jnp.int32(k), r) > 0), k, at)
+        return jnp.where(u >= 4, u + 1, at)
+
+    def slab_of(i, r):
+        return div(i, 2) * NZ + 2 * r + rem(i, 2)
 
     def first(t, s, masked):
         m8 = None
         for g in range(parts):
-            r = score(t, s, g, 0, masked)
-            m8 = r if m8 is None else jnp.maximum(m8, r)
+            v = score(t, s, g, 0, masked)
+            m8 = v if m8 is None else jnp.maximum(m8, v)
         return m8
 
-    zero = jnp.int32(0)
-    m8 = lax.cond(last_slab(zero) == 0, lambda: first(zero, zero, True), lambda: first(zero, zero, False))
-
-    def pair(i, carry):
-        t, s, m8 = carry
-        for u in range(2):
-            done = s == last_slab(t)
-            tn = jnp.where(done, lax.min(t + 1, TILES - 1), t)
-            sn = jnp.where(done, 0, s + 1)
-            m8 = lax.cond(
-                sn == last_slab(tn),
-                lambda m8=m8, u=u, t=t, s=s, tn=tn, sn=sn: item(t, s, tn, sn, m8, u, True),
-                lambda m8=m8, u=u, t=t, s=s, tn=tn, sn=sn: item(t, s, tn, sn, m8, u, False),
-            )
-
-            @pl.when(done)
-            def _(t=t):
-                finish(t)
-
-            t, s = tn, sn
-        return t, s, m8
-
-    lax.fori_loop(0, div(count, 2), pair, (zero, zero, m8))
+    def one_round(r, _):
+        ref = kv.at[:, :, pl.ds(2 * r, 2), :, oc]
+        remote(ref, ref, csend.at[r, 0], crecv.at[r], device(x, y, z, oc)).wait_recv()
+        u0 = following(jnp.int32(-1), r)
+        t0 = tile_at(u0)
+        s0 = slab_of(jnp.int32(0), r)
+        m8 = lax.cond(s0 == last_slab(t0), lambda: first(t0, s0, True), lambda: first(t0, s0, False))
+        count = jnp.int32(0)
+        for k in range(TILES):
+            count = count + steps(jnp.int32(k), r)
+        base = span + every * r
+
+        def pair(i, carry):
+            u, k, m8 = carry
+            slots(lax.min(base + 2 * i, base + every), lax.min(base + 2 * i + 2, base + every))
+            for h in range(2):
+                t, s = tile_at(u), slab_of(k, r)
+                done = k + 1 == steps(u, r)
+                un = jnp.where(done, following(u, r), u)
+                kn = jnp.where(done, 0, k + 1)
+                over = un >= TILES
+                tn = jnp.where(over, t, tile_at(un))
+                sn = jnp.where(over, s, slab_of(kn, r))
+                live = u < TILES
+                masked = jnp.where(sn == last_slab(tn), 1, 0)
+                m8 = lax.switch(
+                    jnp.where(live, masked, 2),
+                    [
+                        lambda m8=m8, h=h, a=(t, s, tn, sn): item(*a, m8, h, False),
+                        lambda m8=m8, h=h, a=(t, s, tn, sn): item(*a, m8, h, True),
+                        lambda m8=m8: m8,
+                    ],
+                )
+                final = jnp.where(u >= 4, ROUNDS - 1, div(pick(rem(u, 4)), 2))
+
+                @pl.when(live & done & (r == final))
+                def _(t=t):
+                    finish(t)
+
+                u, k = un, kn
+            return u, k, m8
+
+        pairs = div(count + 1, 2)
+        lax.fori_loop(0, pairs, pair, (u0, jnp.int32(0), m8))
+        slots(lax.min(base + 2 * pairs, base + every), base + every)
+        return 0
+
+    lax.fori_loop(0, ROUNDS, one_round, 0)
     o_ref[:, o_cols(0)] = o_stage[0, c]
 
     for tile in range(TILES):
@@ -394,8 +461,15 @@
                         o_stage.at[tile, c], o_ref.at[:, cols], osend.at[tile, c], orecv.at[tile, cs[k]],
                         device(x, ys[yy], tz[j], cs[k]),
                     ).wait_recv()
-    for copy in sends:
-        copy.wait_send()
+
+    def sent(r, _):
+        for _, outs, where in numbered:
+            for i, o in outs:
+                g_copy(r, i, *o).wait_send()
+            c_copy(r, *where).wait_send()
+        return 0
+
+    lax.fori_loop(0, ROUNDS, sent, 0)
     for dz in z_order:
         for n in range(2):
             z_copy(dz, n).wait_send()
@@ -429,8 +503,8 @@
             dma((5,)),
             dma((2, NZ)), dma((2, NZ)),
             dma((16,)), dma((TILES, 2)),
-            dma((36,)), dma((4, 4, 2)),
-            dma((2, 8)), dma((2, 8)),
+            dma((ROUNDS, 20)), dma((ROUNDS, 4, 4, 2)),
+            dma((ROUNDS, 16)), dma((ROUNDS,)),
             dma((TILES, 2)), dma((TILES, 2)),
         ],
         compiler_params=pltpu.CompilerParams(

time: 91.9 us -> 89.5 us (0.974)
  the two profiles are of different devices: /device:TPU:1 before, /device:TPU:25 now
where the time goes in v2:
time: 89.5 us; the launch traced here: 89.4 us
  Pallas kernels  88.6 us (99%)
    pallas_call x1, Pallas kernels, per_device(): pl.pallas_call(kernel, out_shape=pltpu.VMEM(queries.shape, queries.dtype)...  88.6 us

profile of v2, /device:TPU:25, one launch (start us, length us, event | category | flops | bytes accessed | tf_op | source)
XLA Modules:
  0.0 89.4 jit_solution(6163201145462431103)
XLA Ops:
  0.0 88.6 %regrouped_attention.1 = bf16[64,4096]{1,0:T(8,128)(2,1)S(1)} custom-call(bf16[64,4096]{1,0:T(8,128)(2,1)} %q_hbm.1, bf16[64,512]{1,0:T(8,128)(2,1)} %k_hbm.1, bf16[64,512]{1,0:T(8,128)(2,1)} %v_hbm.1), custom_call_target="tpu_custom_call" | custom-call | tf_op jit(solution)/shard_map/regrouped_attention/pallas_call | solution.py:486
  88.6 0.8 copy.5

commit v3 on v1

--- a/solution.py
+++ b/solution.py
@@ -16,6 +16,8 @@
 TILES = 8
 SLAB = 1024
 CHUNK = 256
+BLOCKS = NX * NY
+PACE = 2
 SCALE = math.log2(math.e) / math.sqrt(DH)
 ZI_OF = (0, 2, 1, 3)
 f32 = jnp.float32
@@ -120,19 +122,21 @@
     def z_copy(dz, n):
         zz = rem(z + dz, NZ)
         return remote(
-            own[n].at[:, kv_cols(zz)], kv.at[n, yhi, z, blk, c], zsend.at[n, dz], zrecv.at[n, dz], device(x, y, zz, c)
-        )
-
-    def z_landed(dz, n):
-        zz = rem(z + NZ - dz, NZ)
+            own[n].at[:, kv_cols(zz)], kv.at[n, yhi, z, blk, c], zsend.at[n, dz], zrecv.at[n, z], device(x, y, zz, c)
+        )
+
+    def z_landed(zz, n):
         remote(
-            own[n].at[:, kv_cols(z)], kv.at[n, yhi, zz, blk, c], zsend.at[n, dz], zrecv.at[n, dz], device(x, y, zz, c)
+            own[n].at[:, kv_cols(z)], kv.at[n, yhi, zz, blk, c], zsend.at[n, 0], zrecv.at[n, zz], device(x, y, zz, c)
         ).wait_recv()
 
     z_order = (4, 3, 5, 2, 6, 1, 7)
-    for dz in z_order:
-        for n in range(2):
-            z_copy(dz, n).start()
+
+    def z_start():
+        for dz in z_order:
+            for n in range(2):
+                z_copy(dz, n).start()
+
     for load in kept:
         load.wait()
 
@@ -156,109 +160,107 @@
             device(x, ys[yy], zz, cs[k]),
         ).wait_recv()
 
-    for yy in (1, 0):
-        for j in (3, 1, 2, 0):
-            for k in range(2):
-                if j or yy or k:
-                    q_copy(j, yy, k).start()
+    def q_start():
+        for yy in (1, 0):
+            for j in (3, 1, 2, 0):
+                for k in range(2):
+                    if j or yy or k:
+                        q_copy(j, yy, k).start()
+
+    z_start()
+    q_start()
+
     q_in[0, c] = q_own[:, q_cols(0, 0, 0)]
 
-    for dz in z_order:
-        for n in range(2):
-            z_landed(dz, n)
-
-    def a_dev(d):
-        return device(rem(x + d * (1 - c), NX), rem(y + d * c, NY), z, c)
-
-    def b_dev(d):
-        return device(rem(x + d * c, NX), rem(y + d * (1 - c), NY), z, c)
-
-    def block(ra, rb):
-        xk = rem(x + ra * (1 - c) + rb * c, NX)
-        yk = rem(y + ra * c + rb * (1 - c), NY)
+    din = 1 + 2 * rem(y, 2)
+    dys = (0, din, NY - din, 2)
+    IN, OUT, FAR = 1, 2, 3
+    XUP, XDOWN, YIN, YOUT = range(4)
+    to = (
+        device(rem(x + 1, NX), y, z, c), device(rem(x + 3, NX), y, z, c),
+        device(x, rem(y + dys[IN], NY), z, c), device(x, rem(y + dys[OUT], NY), z, c),
+    )
+    order = (
+        (0, 0), (3, 0), (1, 0), (0, IN), (0, OUT), (2, 0), (3, IN), (1, IN),
+        (3, OUT), (1, OUT), (2, IN), (2, OUT), (0, FAR), (3, FAR), (1, FAR), (2, FAR),
+    )
+
+    def block(dx, dy):
+        xk = rem(x + dx, NX)
+        yk = rem(y + dy, NY)
         return div(yk, 2), rem(yk, 2) * 4 + xk
 
-    def piece(ra, rb, n, core):
-        yh, q = block(ra, rb)
+    def piece(dx, sy, n, core):
+        yh, q = block(dx, dys[sy])
         if n is None:
             return kv.at[:, yh, :, q, core]
         return kv.at[n, yh, :, q, core]
 
-    def g_copy(index, ra, rb, n, axis, d):
-        ref = piece(ra, rb, n, c)
-        to = a_dev(d % 4) if axis == 0 else b_dev(d % 4)
-        if axis == 0:
-            there = ((ra - d) % 4, rb)
-        else:
-            there = (ra, (rb - d) % 4)
-        return remote(ref, ref, gsend.at[index], grecv.at[there[0], there[1], n or 0], to)
-
-    def g_landed(ra, rb, n):
-        ref = piece(ra, rb, n, c)
-        remote(ref, ref, gsend.at[0], grecv.at[ra, rb, n or 0], a_dev(1)).wait_recv()
-
-    def c_copy(ra, rb):
-        yh, q = block(ra, rb)
-        ref = piece(ra, rb, None, c)
-        return remote(ref, ref, csend.at[yh, q], crecv.at[yh, q], device(x, y, z, oc))
-
-    sends = []
-
-    def send(copy):
-        copy.start()
-        sends.append(copy)
-
-    def g_send(*what):
-        send(g_copy(len(g_list), *what))
-        g_list.append(what)
-
-    g_list = []
-
-    def spread(ra, rb, axis):
-        for d in (1, -1):
-            g_send(ra, rb, None, axis, d)
-
-    spread(0, 0, 0)
-    spread(0, 0, 1)
-    send(c_copy(0, 0))
-
-    def line(ra, rb, axis, then):
-        for d, n in ((1, 0), (-1, 1)):
-            here = ((ra - d) % 4, rb) if axis == 0 else (ra, (rb - d) % 4)
-            g_landed(*here, None)
-            g_send(*here, n, axis, d)
-            if then:
-                spread(*here, 1)
-            send(c_copy(*here))
-        far = ((ra + 2) % 4, rb) if axis == 0 else (ra, (rb + 2) % 4)
-        return far
-
-    def far_landed(far, then):
-        g_landed(*far, 0)
-        g_landed(*far, 1)
-        if then:
-            spread(*far, 1)
-        send(c_copy(*far))
-
-    far_a = line(0, 0, 0, True)
-    far_b = line(0, 0, 1, False)
-    far_landed(far_a, True)
-    far_landed(far_b, False)
-    for ra in (3, 1, 2):
-        far_landed(line(ra, 0, 1, False), False)
-
-    for yh in range(2):
-        for q in range(8):
-            ref = kv.at[:, yh, :, q, oc]
-            remote(ref, ref, csend.at[yh, q], crecv.at[yh, q], device(x, y, z, oc)).wait_recv()
-
-    for tile in range(TILES):
-        for k in range(2):
-            if tile or k:
-                q_landed(tile, k)
-        for h in range(2):
-            part = q_in[tile, :, :, h * DH : (h + 1) * DH].reshape(2 * 64, DH)
-            qt[tile, :, h * DH : (h + 1) * DH] = part.T
+    def plan(core):
+        made = {}
+        for dx, sy in order:
+            outs = []
+            if (dx, sy) == (0, 0):
+                outs += [(None, XUP, (3, 0)), (None, XDOWN, (1, 0)), (None, YIN, (0, IN)), (None, YOUT, (0, OUT))]
+            if dx in (3, 1) and (core == 1 or sy == 0):
+                outs.append((0, XUP, (2, sy)) if dx == 3 else (1, XDOWN, (2, sy)))
+            if core == 0 and sy == 0 and dx:
+                outs += [(None, YIN, (dx, IN)), (None, YOUT, (dx, OUT))]
+            if core == 1 and dx == 0 and sy:
+                outs += [(None, XUP, (3, sy)), (None, XDOWN, (1, sy))]
+            if (core == 0 or dx == 0) and sy in (IN, OUT):
+                outs.append((0, YOUT, (dx, FAR)) if sy == IN else (1, YIN, (dx, FAR)))
+            if core == 0:
+                halves = sy == FAR or (dx, sy) == (2, 0)
+            else:
+                halves = dx == 2 or (dx, sy) == (0, FAR)
+            made[dx, sy] = (halves, outs)
+        return made
+
+    def g_copy(where, i, n, via, there):
+        ref = piece(*where, n, c)
+        return remote(ref, ref, gsend.at[i], grecv.at[there[0], there[1], n or 0], to[via])
+
+    def g_copies(core):
+        found, i = {}, 0
+        for where, (halves, outs) in plan(core).items():
+            found[where] = (halves, [])
+            for n, via, there in outs:
+                found[where][1].append((i, n, via, there))
+                i += 1
+        return found
+
+    def c_copy(p):
+        ref = piece(*order[p], None, c)
+        return remote(ref, ref, csend.at[p], crecv.at[p], device(x, y, z, oc))
+
+    def event(p):
+        where = order[p]
+        for core in range(2):
+            @pl.when(c == core)
+            def _(core=core):
+                halves, outs = g_copies(core)[where]
+                if p:
+                    for n in (0, 1) if halves else (None,):
+                        ref = piece(*where, n, c)
+                        remote(ref, ref, gsend.at[0], grecv.at[where[0], where[1], n or 0], to[0]).wait_recv()
+                for out in outs:
+                    g_copy(where, *out).start()
+        c_copy(p).start()
+
+    for dz in range(1, NZ):
+        for n in range(2):
+            z_landed(rem(z + dz, NZ), n)
+
+    def take_queries():
+        for tile in range(TILES):
+            for k in range(2):
+                if tile or k:
+                    q_landed(tile, k)
+            for h in range(2):
+                part = q_in[tile, :, :, h * DH : (h + 1) * DH].reshape(2 * 64, DH)
+                qt[tile, :, h * DH : (h + 1) * DH] = part.T
+
     mx[...] = jnp.full(mx.shape, -jnp.inf, f32)
     tot[...] = jnp.zeros(tot.shape, f32)
     acc[...] = jnp.zeros(acc.shape, f32)
@@ -267,10 +269,12 @@
         side = jnp.where(t < 4, yhi, 1 - yhi)
         return side * NZ + zsrc(z, rem(t, 4))
 
-    def segment(n, s, g):
-        yh = div(s, NZ)
-        zz = rem(s, NZ)
-        return jnp.concatenate([kv[n, yh, zz, 2 * g + i].reshape(2 * 64, DH) for i in range(2)], axis=0)
+    def segment(n, at, g):
+        yh, z0, dz, q0, dq = at
+        rows = []
+        for i in range(2 * g, 2 * g + 2):
+            rows.append(kv[n, yh, z0 + i * dz, q0 + i * dq].reshape(2 * 64, DH))
+        return jnp.concatenate(rows, axis=0)
 
     def fold(v, op):
         return op(v.reshape(v.shape[0] // 8, 8, v.shape[1]), axis=0)
@@ -341,40 +345,127 @@
         tot[t] = l8
         return nm
 
-    count = 0
-    for t in range(TILES):
-        count = count + last_slab(jnp.int32(t)) + 1
-
-    def first(t, s, masked):
+    near = [zsrc(z, i) for i in range(4)]
+
+    def choose(i, values):
+        got = jnp.int32(values[-1])
+        for k in range(len(values) - 1):
+            got = jnp.where(i == k, values[k], got)
+        return got
+
+    def cross_address(p):
+        dx = choose(p, [dx for dx, _ in order])
+        sy = choose(p, [sy for _, sy in order])
+        yh, q = block(dx, choose(sy, dys))
+        return yh, jnp.int32(0), jnp.int32(1), q, jnp.int32(0)
+
+    late_start = 4 * yhi
+    late = 4 * (1 - yhi)
+
+    def first(t, at, masked):
         m8 = None
         for g in range(parts):
-            r = score(t, s, g, 0, masked)
-            m8 = r if m8 is None else jnp.maximum(m8, r)
+            v = score(t, at, g, 0, masked)
+            m8 = v if m8 is None else jnp.maximum(m8, v)
         return m8
 
+    def other(p):
+        yh, q = block(choose(p, [dx for dx, _ in order]), choose(choose(p, [sy for _, sy in order]), dys))
+        ref = kv.at[:, yh, :, q, oc]
+        remote(ref, ref, csend.at[p], crecv.at[p], device(x, y, z, oc)).wait_recv()
+
+    def relay(lo, hi):
+        def step(p, _):
+            lax.switch(p, [functools.partial(event, i) for i in range(BLOCKS)])
+            return 0
+
+        lax.fori_loop(lo, hi, step, 0)
+
+    def others(lo, hi):
+        lax.fori_loop(lo, hi, lambda p, _: (other(p), 0)[1], 0)
+
+    relay(0, 5)
+    take_queries()
+    others(0, 5)
+
+    def about(p):
+        dx = choose(p, [dx for dx, _ in order])
+        sy = choose(p, [sy for _, sy in order])
+        _, q = block(dx, choose(sy, dys))
+        early = jnp.where(yhi == 0, sy < 2, sy >= 2)
+        nc = jnp.where((p < 16) & early, 4, 0)
+        far_turn = p >= 16
+        own_turn = (p >= 10) & (p < 14)
+        ts = jnp.where(far_turn, 23 - p, jnp.where(own_turn, p - 10, 0))
+        slabs = jnp.where(far_turn | own_turn, choose(rem(ts, 4), near) + 1, 0)
+        return p, nc, q, ts, nc + slabs
+
+    def after(p):
+        skip = jnp.where(
+            yhi == 0, jnp.where((p == 7) | (p == 13), 3, jnp.where(p == 3, 2, 1)), jnp.where(p == 4, 4, 1)
+        )
+        return p + skip
+
+    def what(k, stage):
+        p, nc, q, ts, n = stage
+        crosses = k < nc
+        t = jnp.where(crosses, late + k, ts)
+        side = jnp.where(ts < 4, yhi, 1 - yhi)
+        dz = jnp.where(crosses, 1, 0)
+        at = (
+            jnp.where(crosses, 0, side), jnp.where(crosses, 0, k - nc), dz, jnp.where(crosses, q, 0), 1 - dz,
+        )
+        return t, at, (k + 1 == n) & (n != nc)
+
     zero = jnp.int32(0)
-    m8 = lax.cond(last_slab(zero) == 0, lambda: first(zero, zero, True), lambda: first(zero, zero, False))
+    stage0 = about(late_start)
+    t0, at0, _ = what(zero, stage0)
+    m8 = first(t0, at0, False)
+    total = 40 + 2 * (near[0] + near[1] + near[2] + near[3])
+
+    def advance(i, stage, ran, had):
+        p = stage[0]
+        pn = lax.min(after(p), 19)
+        due = lax.max(ran, lax.min(lax.max(5 + div(i, PACE), pn + 1), BLOCKS))
+        relay(ran, due)
+        seen = lax.max(had, lax.min(pn + 1, BLOCKS))
+        others(had, seen)
+        return about(pn), due, seen
+
+    def ended(p, ts):
+        @pl.when((p >= 16) | ((p >= 10) & (p < 14) & (yhi == 0)))
+        def _():
+            finish(ts)
+
+        @pl.when((p == 15) & (yhi == 1))
+        def _():
+            lax.fori_loop(0, 4, lambda t, _: (finish(t), 0)[1], 0)
 
     def pair(i, carry):
-        t, s, m8 = carry
-        for u in range(2):
-            done = s == last_slab(t)
-            tn = jnp.where(done, lax.min(t + 1, TILES - 1), t)
-            sn = jnp.where(done, 0, s + 1)
+        k, stage, ran, had, t, at, m8 = carry
+        for h in range(2):
+            last = k + 1 == stage[4]
+            more, ran, had = lax.cond(
+                last,
+                lambda stage=stage, ran=ran, had=had: advance(i, stage, ran, had),
+                lambda stage=stage, ran=ran, had=had: (stage, ran, had),
+            )
+            kn = jnp.where(last, 0, k + 1)
+            tn, an, diag = what(kn, more)
             m8 = lax.cond(
-                sn == last_slab(tn),
-                lambda m8=m8, u=u, t=t, s=s, tn=tn, sn=sn: item(t, s, tn, sn, m8, u, True),
-                lambda m8=m8, u=u, t=t, s=s, tn=tn, sn=sn: item(t, s, tn, sn, m8, u, False),
+                diag,
+                lambda m8=m8, h=h, a=(t, at, tn, an): item(*a, m8, h, True),
+                lambda m8=m8, h=h, a=(t, at, tn, an): item(*a, m8, h, False),
             )
 
-            @pl.when(done)
-            def _(t=t):
-                finish(t)
-
-            t, s = tn, sn
-        return t, s, m8
-
-    lax.fori_loop(0, div(count, 2), pair, (zero, zero, m8))
+            @pl.when(last)
+            def _(stage=stage):
+                ended(stage[0], stage[3])
+
+            k, stage, t, at = kn, more, tn, an
+        return k, stage, ran, had, t, at, m8
+
+    lax.fori_loop(0, div(total, 2), pair, (zero, stage0, zero + 5, zero + 5, t0, at0, m8))
     o_ref[:, o_cols(0)] = o_stage[0, c]
 
     for tile in range(TILES):
@@ -394,8 +485,16 @@
                         o_stage.at[tile, c], o_ref.at[:, cols], osend.at[tile, c], orecv.at[tile, cs[k]],
                         device(x, ys[yy], tz[j], cs[k]),
                     ).wait_recv()
-    for copy in sends:
-        copy.wait_send()
+
+    for core in range(2):
+        @pl.when(c == core)
+        def _(core=core):
+            for where, (_, outs) in g_copies(core).items():
+                for out in outs:
+                    g_copy(where, *out).wait_send()
+
+    for p in range(len(order)):
+        c_copy(p).wait_send()
     for dz in z_order:
         for n in range(2):
             z_copy(dz, n).wait_send()
@@ -429,8 +528,8 @@
             dma((5,)),
             dma((2, NZ)), dma((2, NZ)),
             dma((16,)), dma((TILES, 2)),
-            dma((36,)), dma((4, 4, 2)),
-            dma((2, 8)), dma((2, 8)),
+            dma((24,)), dma((4, 4, 2)),
+            dma((16,)), dma((16,)),
             dma((TILES, 2)), dma((TILES, 2)),
         ],
         compiler_params=pltpu.CompilerParams(

time: 91.9 us -> 82.2 us (0.89)
  Pallas kernels: 91 us -> 81.3 us
    pallas_call x1, Pallas kernels: 91 us -> 81.3 us  [per_device(): pl.pallas_call(kernel, out_shape=pltpu.VMEM(queries.shape, queries.dtype)...]
where the time goes in v3:
time: 82.2 us; the launch traced here: 82.1 us
  Pallas kernels  81.3 us (99%)
    pallas_call x1, Pallas kernels, per_device(): pl.pallas_call(kernel, out_shape=pltpu.VMEM(queries.shape, queries.dtype)...  81.3 us

profile of v3, /device:TPU:1, one launch (start us, length us, event | category | flops | bytes accessed | tf_op | source)
XLA Modules:
  0.0 82.1 jit_solution(15355038961861630877)
XLA Ops:
  0.0 81.3 %regrouped_attention.1 = bf16[64,4096]{1,0:T(8,128)(2,1)S(1)} custom-call(bf16[64,4096]{1,0:T(8,128)(2,1)} %q_hbm.1, bf16[64,512]{1,0:T(8,128)(2,1)} %k_hbm.1, bf16[64,512]{1,0:T(8,128)(2,1)} %v_hbm.1), custom_call_target="tpu_custom_call" | custom-call | tf_op jit(solution)/shard_map/regrouped_attention/pallas_call | solution.py:511
  81.3 0.8 copy.5

commit v4 on v3

--- a/solution.py
+++ b/solution.py
@@ -15,9 +15,10 @@
 NX, NY, NZ = 4, 4, 8
 TILES = 8
 SLAB = 1024
-CHUNK = 256
+CHUNK = 512
 BLOCKS = NX * NY
-PACE = 2
+PACE = 1
+FIRST = 5
 SCALE = math.log2(math.e) / math.sqrt(DH)
 ZI_OF = (0, 2, 1, 3)
 f32 = jnp.float32
@@ -180,9 +181,15 @@
         device(rem(x + 1, NX), y, z, c), device(rem(x + 3, NX), y, z, c),
         device(x, rem(y + dys[IN], NY), z, c), device(x, rem(y + dys[OUT], NY), z, c),
     )
-    order = (
-        (0, 0), (3, 0), (1, 0), (0, IN), (0, OUT), (2, 0), (3, IN), (1, IN),
-        (3, OUT), (1, OUT), (2, IN), (2, OUT), (0, FAR), (3, FAR), (1, FAR), (2, FAR),
+    orders = (
+        (
+            (0, 0), (3, 0), (1, 0), (0, IN), (2, 0), (3, IN), (1, IN), (0, OUT),
+            (2, IN), (3, OUT), (1, OUT), (2, OUT), (0, FAR), (3, FAR), (1, FAR), (2, FAR),
+        ),
+        (
+            (0, 0), (0, OUT), (3, 0), (1, 0), (3, OUT), (1, OUT), (0, IN), (0, FAR),
+            (2, 0), (2, OUT), (3, FAR), (1, FAR), (2, FAR), (3, IN), (1, IN), (2, IN),
+        ),
     )
 
     def block(dx, dy):
@@ -198,7 +205,7 @@
 
     def plan(core):
         made = {}
-        for dx, sy in order:
+        for dx, sy in orders[0]:
             outs = []
             if (dx, sy) == (0, 0):
                 outs += [(None, XUP, (3, 0)), (None, XDOWN, (1, 0)), (None, YIN, (0, IN)), (None, YOUT, (0, OUT))]
@@ -230,23 +237,36 @@
                 i += 1
         return found
 
-    def c_copy(p):
-        ref = piece(*order[p], None, c)
+    def choose(i, values):
+        got = jnp.int32(values[-1])
+        for k in range(len(values) - 1):
+            got = jnp.where(i == k, values[k], got)
+        return got
+
+    def place(p):
+        dx, sy = (
+            jnp.where(yhi == 0, *(choose(p, [where[n] for where in order]) for order in orders)) for n in range(2)
+        )
+        return dx, sy, block(dx, choose(sy, dys))
+
+    def c_copy(p, core):
+        yh, q = place(p)[2]
+        ref = kv.at[:, yh, :, q, core]
         return remote(ref, ref, csend.at[p], crecv.at[p], device(x, y, z, oc))
 
     def event(p):
-        where = order[p]
-        for core in range(2):
-            @pl.when(c == core)
-            def _(core=core):
-                halves, outs = g_copies(core)[where]
-                if p:
-                    for n in (0, 1) if halves else (None,):
-                        ref = piece(*where, n, c)
-                        remote(ref, ref, gsend.at[0], grecv.at[where[0], where[1], n or 0], to[0]).wait_recv()
-                for out in outs:
-                    g_copy(where, *out).start()
-        c_copy(p).start()
+        for half in range(2):
+            for core in range(2):
+                @pl.when((c == core) & (yhi == half))
+                def _(core=core, half=half):
+                    where = orders[half][p]
+                    halves, outs = g_copies(core)[where]
+                    if p:
+                        for n in (0, 1) if halves else (None,):
+                            ref = piece(*where, n, c)
+                            remote(ref, ref, gsend.at[0], grecv.at[where[0], where[1], n or 0], to[0]).wait_recv()
+                    for out in outs:
+                        g_copy(where, *out).start()
 
     for dz in range(1, NZ):
         for n in range(2):
@@ -272,7 +292,7 @@
     def segment(n, at, g):
         yh, z0, dz, q0, dq = at
         rows = []
-        for i in range(2 * g, 2 * g + 2):
+        for i in range(CHUNK // DH * g, CHUNK // DH * (g + 1)):
             rows.append(kv[n, yh, z0 + i * dz, q0 + i * dq].reshape(2 * 64, DH))
         return jnp.concatenate(rows, axis=0)
 
@@ -347,19 +367,7 @@
 
     near = [zsrc(z, i) for i in range(4)]
 
-    def choose(i, values):
-        got = jnp.int32(values[-1])
-        for k in range(len(values) - 1):
-            got = jnp.where(i == k, values[k], got)
-        return got
-
-    def cross_address(p):
-        dx = choose(p, [dx for dx, _ in order])
-        sy = choose(p, [sy for _, sy in order])
-        yh, q = block(dx, choose(sy, dys))
-        return yh, jnp.int32(0), jnp.int32(1), q, jnp.int32(0)
-
-    late_start = 4 * yhi
+    start = yhi
     late = 4 * (1 - yhi)
 
     def first(t, at, masked):
@@ -369,40 +377,37 @@
             m8 = v if m8 is None else jnp.maximum(m8, v)
         return m8
 
-    def other(p):
-        yh, q = block(choose(p, [dx for dx, _ in order]), choose(choose(p, [sy for _, sy in order]), dys))
-        ref = kv.at[:, yh, :, q, oc]
-        remote(ref, ref, csend.at[p], crecv.at[p], device(x, y, z, oc)).wait_recv()
-
     def relay(lo, hi):
         def step(p, _):
             lax.switch(p, [functools.partial(event, i) for i in range(BLOCKS)])
+            c_copy(p, c).start()
             return 0
 
         lax.fori_loop(lo, hi, step, 0)
 
     def others(lo, hi):
-        lax.fori_loop(lo, hi, lambda p, _: (other(p), 0)[1], 0)
-
-    relay(0, 5)
+        lax.fori_loop(lo, hi, lambda p, _: (c_copy(p, oc).wait_recv(), 0)[1], 0)
+
+    relay(0, 4)
     take_queries()
-    others(0, 5)
+    others(0, 4)
+
+    whole = 9 + 3 * yhi
 
     def about(p):
-        dx = choose(p, [dx for dx, _ in order])
-        sy = choose(p, [sy for _, sy in order])
-        _, q = block(dx, choose(sy, dys))
+        _, sy, (_, q) = place(p)
         early = jnp.where(yhi == 0, sy < 2, sy >= 2)
         nc = jnp.where((p < 16) & early, 4, 0)
-        far_turn = p >= 16
-        own_turn = (p >= 10) & (p < 14)
-        ts = jnp.where(far_turn, 23 - p, jnp.where(own_turn, p - 10, 0))
-        slabs = jnp.where(far_turn | own_turn, choose(rem(ts, 4), near) + 1, 0)
-        return p, nc, q, ts, nc + slabs
+        second = p >= 16
+        slabs = second | ((p >= whole) & (p < whole + 4))
+        ts = jnp.where(second, late + 19 - p, jnp.where(slabs, 4 - late + p - whole, 0))
+        return p, nc, q, ts, nc + jnp.where(slabs, choose(rem(ts, 4), near) + 1, 0)
 
     def after(p):
         skip = jnp.where(
-            yhi == 0, jnp.where((p == 7) | (p == 13), 3, jnp.where(p == 3, 2, 1)), jnp.where(p == 4, 4, 1)
+            yhi == 0,
+            jnp.where(p == 6, 2, jnp.where(p == 12, 4, 1)),
+            jnp.where(p == 1, 3, jnp.where((p == 5) | (p == 7), 2, 1)),
         )
         return p + skip
 
@@ -418,7 +423,7 @@
         return t, at, (k + 1 == n) & (n != nc)
 
     zero = jnp.int32(0)
-    stage0 = about(late_start)
+    stage0 = about(start)
     t0, at0, _ = what(zero, stage0)
     m8 = first(t0, at0, False)
     total = 40 + 2 * (near[0] + near[1] + near[2] + near[3])
@@ -426,20 +431,11 @@
     def advance(i, stage, ran, had):
         p = stage[0]
         pn = lax.min(after(p), 19)
-        due = lax.max(ran, lax.min(lax.max(5 + div(i, PACE), pn + 1), BLOCKS))
+        due = lax.max(ran, lax.min(lax.max(FIRST + div(i, PACE), pn + 1), BLOCKS))
         relay(ran, due)
         seen = lax.max(had, lax.min(pn + 1, BLOCKS))
         others(had, seen)
         return about(pn), due, seen
-
-    def ended(p, ts):
-        @pl.when((p >= 16) | ((p >= 10) & (p < 14) & (yhi == 0)))
-        def _():
-            finish(ts)
-
-        @pl.when((p == 15) & (yhi == 1))
-        def _():
-            lax.fori_loop(0, 4, lambda t, _: (finish(t), 0)[1], 0)
 
     def pair(i, carry):
         k, stage, ran, had, t, at, m8 = carry
@@ -458,14 +454,14 @@
                 lambda m8=m8, h=h, a=(t, at, tn, an): item(*a, m8, h, False),
             )
 
-            @pl.when(last)
+            @pl.when(last & (stage[4] > stage[1]))
             def _(stage=stage):
-                ended(stage[0], stage[3])
+                finish(stage[3])
 
             k, stage, t, at = kn, more, tn, an
         return k, stage, ran, had, t, at, m8
 
-    lax.fori_loop(0, div(total, 2), pair, (zero, stage0, zero + 5, zero + 5, t0, at0, m8))
+    lax.fori_loop(0, div(total, 2), pair, (zero, stage0, zero + 4, zero + 4, t0, at0, m8))
     o_ref[:, o_cols(0)] = o_stage[0, c]
 
     for tile in range(TILES):
@@ -493,8 +489,7 @@
                 for out in outs:
                     g_copy(where, *out).wait_send()
 
-    for p in range(len(order)):
-        c_copy(p).wait_send()
+    lax.fori_loop(0, BLOCKS, lambda p, _: (c_copy(p, c).wait_send(), 0)[1], 0)
     for dz in z_order:
         for n in range(2):
             z_copy(dz, n).wait_send()

time: 82.2 us -> 80.4 us (0.978)
  Pallas kernels: 81.3 us -> 79.5 us
    pallas_call x1, Pallas kernels: 81.3 us -> 79.5 us  [per_device(): pl.pallas_call(kernel, out_shape=pltpu.VMEM(queries.shape, queries.dtype)...]
where the time goes in v4:
time: 80.4 us; the launch traced here: 80.3 us
  Pallas kernels  79.5 us (99%)
    pallas_call x1, Pallas kernels, per_device(): pl.pallas_call(kernel, out_shape=pltpu.VMEM(queries.shape, queries.dtype)...  79.5 us

profile of v4, /device:TPU:1, one launch (start us, length us, event | category | flops | bytes accessed | tf_op | source)
XLA Modules:
  0.0 80.3 jit_solution(12335971793461092561)
XLA Ops:
  0.0 79.5 %regrouped_attention.1 = bf16[64,4096]{1,0:T(8,128)(2,1)S(1)} custom-call(bf16[64,4096]{1,0:T(8,128)(2,1)} %q_hbm.1, bf16[64,512]{1,0:T(8,128)(2,1)} %k_hbm.1, bf16[64,512]{1,0:T(8,128)(2,1)} %v_hbm.1), custom_call_target="tpu_custom_call" | custom-call | tf_op jit(solution)/shard_map/regrouped_attention/pallas_call | solution.py:506
  79.5 0.8 copy.5

commit v5 on v4

--- a/solution.py
+++ b/solution.py
@@ -113,6 +113,10 @@
     ):
         greet(where)
         greeted += 1
+
+    mx[...] = jnp.full(mx.shape, -jnp.inf, f32)
+    tot[...] = jnp.zeros(tot.shape, f32)
+    acc[...] = jnp.zeros(acc.shape, f32)
 
     for load in loads:
         load.wait()
@@ -281,9 +285,6 @@
                 part = q_in[tile, :, :, h * DH : (h + 1) * DH].reshape(2 * 64, DH)
                 qt[tile, :, h * DH : (h + 1) * DH] = part.T
 
-    mx[...] = jnp.full(mx.shape, -jnp.inf, f32)
-    tot[...] = jnp.zeros(tot.shape, f32)
-    acc[...] = jnp.zeros(acc.shape, f32)
 
     def last_slab(t):
         side = jnp.where(t < 4, yhi, 1 - yhi)

time: 80.4 us -> 80.4 us (level)
  no operation moved by 1% of the time
where the time goes in v5:
time: 80.4 us; the launch traced here: 80.3 us
  Pallas kernels  79.5 us (99%)
    pallas_call x1, Pallas kernels, per_device(): pl.pallas_call(kernel, out_shape=pltpu.VMEM(queries.shape, queries.dtype)...  79.5 us

profile of v5, /device:TPU:1, one launch (start us, length us, event | category | flops | bytes accessed | tf_op | source)
XLA Modules:
  0.0 80.3 jit_solution(3761912590846596369)
XLA Ops:
  0.0 79.5 %regrouped_attention.1 = bf16[64,4096]{1,0:T(8,128)(2,1)S(1)} custom-call(bf16[64,4096]{1,0:T(8,128)(2,1)} %q_hbm.1, bf16[64,512]{1,0:T(8,128)(2,1)} %k_hbm.1, bf16[64,512]{1,0:T(8,128)(2,1)} %v_hbm.1), custom_call_target="tpu_custom_call" | custom-call | tf_op jit(solution)/shard_map/regrouped_attention/pallas_call | solution.py:507
  79.5 0.8 copy.5
